TPU v7x, 32 devices: a whole 2x2x4 slice. The times are simulated.
32 devices in a mesh: rep: 8 (over z, y), shard: 4 (over x, core).
Axes of the slice: x: 2, y: 2, z: 4, core: 2. Of those that a mesh axis runs over, the one named last changes fastest.
Arguments:
- prompt: bfloat16 [8, 1024, 768], P('rep', 'shard'), may hold values from -6 to 6
- conts: bfloat16 [8, 4, 512, 768], P('rep', 'shard'), may hold values from -6 to 6
- prompt_cot: bfloat16 [8, 1024, 768], P('rep', 'shard'), may hold values from -6 to 6
- cont_cot: bfloat16 [8, 4, 512, 768], P('rep', 'shard'), may hold values from -6 to 6
- labels: int32 [8, 4], P('rep', 'shard'), may hold values from 0 to 13
- w_qkv: float32 [768, 2304], P('shard'), may hold values from -0.21875 to 0.21875
- w_out: float32 [768, 768], P('shard'), may hold values from -3.5 to 3.5
- w_in: float32 [768, 3072], P('shard'), may hold values from -0.21875 to 0.21875
- w_ffo: float32 [3072, 768], P('shard'), may hold values from -0.109375 to 0.109375
- layer_biases: float32 [6, 768], replicated, may hold values from -3 to 3
- norm_gains: float32 [2, 768], replicated, may hold values from 0.25 to 1.75
- bias_in: float32 [3072], replicated, may hold values from -3 to 3
- w_student: float32 [768, 128], replicated, may hold values from -0.21875 to 0.21875
- student_vectors: float32 [3, 128], replicated, may hold values from -4 to 4
- w_pool: float32 [128, 128], replicated, may hold values from -0.5 to 0.5
- w_class: float32 [128, 14], replicated, may hold values from -1 to 1
- bias_class: float32 [14], replicated, may hold values from -3 to 3
Outputs:
- prompt_out: bfloat16 [8, 1024, 768], P('rep', 'shard')
- cont_out: bfloat16 [8, 4, 512, 768], P('rep', 'shard')
- logits: float32 [8, 4, 14], P('rep', 'shard')
- prompt_grad: float32 [8, 1024, 768], P('rep', 'shard')
- cont_grad: float32 [8, 4, 512, 768], P('rep', 'shard')
- grad_qkv: float32 [768, 2304], P('shard')
- grad_out: float32 [768, 768], P('shard')
- grad_in: float32 [768, 3072], P('shard')
- grad_ffo: float32 [3072, 768], P('shard')
- grad_biases: float32 [6, 768], replicated
- grad_gains: float32 [2, 768], replicated
- grad_bias_in: float32 [3072], replicated
- grad_student: float32 [768, 128], replicated
- grad_student_vectors: float32 [3, 128], replicated
- grad_pool: float32 [128, 128], replicated
- grad_class: float32 [128, 14], replicated
- grad_bias_class: float32 [14], replicated
All inputs are finite; a program needn't handle non-finite values.
Results may differ from a plain program's by a relative error of at most 0.02.
Values may be sent and summed in bfloat16 or wider, within the bound.
A program may use at most 192 MiB of HBM per device.

v0:
```python
import jax
import jax.numpy as jnp
from jax import lax
from jax.sharding import PartitionSpec as P

D = 768
HEADS = 12
DH = 64
STU = 128
SHEADS = 2


HIGHEST = lax.Precision.HIGHEST
NEG_BIG = -1e30


def dot_plain(left, right):
    return jnp.dot(left, right, preferred_element_type=jnp.float32)


def dot_first(left, right):
    return lax.dot_general(
        left, right, (((0,), (0,)), ((), ())), preferred_element_type=jnp.float32
    )


def dot_second(left, right):
    return lax.dot_general(
        left, right, (((1,), (1,)), ((), ())), preferred_element_type=jnp.float32
    )


def column_slice(matrix, head_index):
    return lax.dynamic_slice_in_dim(matrix, head_index * DH, DH, 1)


def layer_norm(values, gain, shift):
    center = values - jnp.mean(values, -1, keepdims=True)
    spread = jnp.mean(center * center, -1, keepdims=True)
    return center * lax.rsqrt(spread + 1e-05) * gain + shift


def gelu_exact(values):
    return jax.nn.gelu(values, approximate=False)


def attend_forward(queries, keys_all, values_all, allowed):
    scaling = DH ** (-0.5)

    def one_head(head_index):
        scores = jnp.where(
            allowed,
            dot_second(column_slice(queries, head_index), column_slice(keys_all, head_index))
            * scaling,
            NEG_BIG,
        )
        largest = jnp.max(scores, 1, keepdims=True)
        expo = jnp.exp(scores - largest)
        total = jnp.sum(expo, 1, keepdims=True)
        probs = (expo / total).astype(jnp.bfloat16)
        return (
            dot_plain(probs, column_slice(values_all, head_index)),
            (largest + jnp.log(total))[:, 0],
        )

    heads, log_totals = lax.map(one_head, jnp.arange(HEADS))
    return (heads.transpose(1, 0, 2).reshape(queries.shape[0], HEADS * DH), log_totals)


def attend_backward(queries, keys_all, values_all, allowed, grad_att, log_totals):
    scaling = DH ** (-0.5)

    def one_head(item):
        head_index, log_row = item
        query_h = column_slice(queries, head_index)
        key_h = column_slice(keys_all, head_index)
        grad_h = column_slice(grad_att, head_index)
        scores = jnp.where(allowed, dot_second(query_h, key_h) * scaling, NEG_BIG)
        probs = jnp.exp(scores - log_row[:, None])
        grad_probs = dot_second(grad_h, column_slice(values_all, head_index))
        delta = jnp.sum(grad_probs * probs, 1, keepdims=True)
        grad_scores = (probs * (grad_probs - delta)).astype(jnp.bfloat16)
        grad_query = dot_plain(grad_scores, key_h) * scaling
        grad_key = dot_first(grad_scores, query_h) * scaling
        grad_value = dot_first(probs.astype(jnp.bfloat16), grad_h)
        return (grad_query, grad_key, grad_value)

    grad_q, grad_k, grad_v = lax.map(one_head, (jnp.arange(HEADS), log_totals))

    def merge_heads(block):
        return block.transpose(1, 0, 2).reshape(block.shape[1], HEADS * DH)

    return (merge_heads(grad_q), merge_heads(grad_k), merge_heads(grad_v))


def student_loss(stu_rows, pool_query, bias_pool, w_pool, w_class, bias_class, label_value):
    part_w = STU // SHEADS
    parts = stu_rows.reshape(stu_rows.shape[0], SHEADS, part_w)
    queries = pool_query.reshape(SHEADS, part_w)
    scores = jnp.einsum("tha,ha->ht", parts, queries, precision=HIGHEST) * part_w ** (-0.5)
    largest = jnp.max(scores, -1, keepdims=True)
    expo = jnp.exp(scores - largest)
    weights = expo / jnp.sum(expo, -1, keepdims=True)
    pooled = jnp.einsum("ht,tha->ha", weights, parts, precision=HIGHEST).reshape(STU)
    top_layer = jnp.tanh(jnp.dot(pooled, w_pool, precision=HIGHEST) + bias_pool)
    logit_row = jnp.dot(top_layer, w_class, precision=HIGHEST) + bias_class
    top_logit = jnp.max(logit_row)
    log_total = jnp.log(jnp.sum(jnp.exp(logit_row - top_logit))) + top_logit
    picked = jnp.sum(jnp.where(jnp.arange(logit_row.shape[0]) == label_value, logit_row, 0.0))
    return (log_total - picked, logit_row)


def body(
    prompt,
    conts,
    prompt_cot,
    cont_cot,
    labels,
    w_qkv,
    w_out,
    w_in,
    w_ffo,
    layer_biases,
    norm_gains,
    bias_in,
    w_student,
    student_vectors,
    w_pool,
    w_class,
    bias_class,
):
    prompt_rows = prompt.shape[1]
    cont_len = conts.shape[2]
    prompt_len = prompt_rows * lax.axis_size("shard")
    qkv_low = w_qkv.astype(jnp.bfloat16)
    out_low = w_out.astype(jnp.bfloat16)
    in_low = w_in.astype(jnp.bfloat16)
    ffo_low = w_ffo.astype(jnp.bfloat16)
    qkv_full, out_full, in_full, ffo_full = (
        lax.all_gather(qkv_low, "shard", axis=0, tiled=True),
        lax.all_gather(out_low, "shard", axis=0, tiled=True),
        lax.all_gather(in_low, "shard", axis=0, tiled=True),
        lax.all_gather(ffo_low, "shard", axis=0, tiled=True),
    )
    tokens = jnp.concatenate([prompt[0], conts[0, 0]], 0)
    tokens_f = tokens.astype(jnp.float32)
    zero_row = jnp.zeros((D,), jnp.float32)
    bias_three = jnp.concatenate([layer_biases[0], zero_row, layer_biases[1]])
    qkv_b = (dot_plain(tokens, qkv_full) + bias_three).astype(jnp.bfloat16)
    queries = qkv_b[:, :D]
    keys_own = qkv_b[:, D : 2 * D]
    values_own = qkv_b[:, 2 * D :]
    prompt_keys, prompt_values = (
        lax.all_gather(keys_own[:prompt_rows], "shard", axis=0, tiled=True),
        lax.all_gather(values_own[:prompt_rows], "shard", axis=0, tiled=True),
    )
    keys_all = jnp.concatenate([prompt_keys, keys_own[prompt_rows:]], 0)
    values_all = jnp.concatenate([prompt_values, values_own[prompt_rows:]], 0)
    key_pos = jnp.arange(prompt_len + cont_len)
    query_pos = jnp.concatenate(
        [
            lax.axis_index("shard") * prompt_rows + jnp.arange(prompt_rows),
            prompt_len + jnp.arange(cont_len),
        ]
    )
    allowed = key_pos[None, :] <= query_pos[:, None]
    attended, log_totals = attend_forward(queries, keys_all, values_all, allowed)
    att_b = attended.astype(jnp.bfloat16)
    branch = dot_plain(att_b, out_full) + layer_biases[2]
    resid_one = tokens_f + branch
    first = layer_norm(resid_one, norm_gains[0], layer_biases[4])
    first_b = first.astype(jnp.bfloat16)
    hidden = dot_plain(first_b, in_full) + bias_in
    act_b = gelu_exact(hidden).astype(jnp.bfloat16)
    ffn = dot_plain(act_b, ffo_full) + layer_biases[3]
    resid_two = first + ffn
    output = layer_norm(resid_two, norm_gains[1], layer_biases[5])
    output_b = output.astype(jnp.bfloat16)
    cont_b = output_b[prompt_rows:]
    student_low = w_student.astype(jnp.bfloat16)
    stu = dot_plain(cont_b, student_low) + student_vectors[0]

    def loss_closed(stu_rows, pool_query, bias_pool, pool_weight, class_weight, class_bias):
        return student_loss(
            stu_rows, pool_query, bias_pool, pool_weight, class_weight, class_bias, labels[0, 0]
        )

    loss_value, loss_pull, logit_row = jax.vjp(
        loss_closed,
        stu,
        student_vectors[1],
        student_vectors[2],
        w_pool,
        w_class,
        bias_class,
        has_aux=True,
    )
    g_stu, g_query, g_pbias, g_pool, g_class, g_cbias = loss_pull(jnp.ones((), jnp.float32))
    g_stu_b = g_stu.astype(jnp.bfloat16)
    g_sbias = jnp.sum(g_stu_b.astype(jnp.float32), 0)
    g_student = dot_first(cont_b, g_stu_b)
    student_back = dot_second(g_stu_b, student_low)
    g_output = jnp.concatenate([prompt_cot[0], cont_cot[0, 0]], 0).astype(jnp.float32)
    g_output = g_output + jnp.concatenate(
        [jnp.zeros((prompt_rows, D), jnp.float32), student_back], 0
    )
    qkv_back, out_back, in_back, ffo_back = (
        lax.all_gather(qkv_low, "shard", axis=0, tiled=True),
        lax.all_gather(out_low, "shard", axis=0, tiled=True),
        lax.all_gather(in_low, "shard", axis=0, tiled=True),
        lax.all_gather(ffo_low, "shard", axis=0, tiled=True),
    )
    norm_two, norm_two_pull = jax.vjp(layer_norm, resid_two, norm_gains[1], layer_biases[5])
    g_resid_two, g_gain_two, g_shift_two = norm_two_pull(g_output)
    g_ffn_b = g_resid_two.astype(jnp.bfloat16)
    g_ffo = dot_first(act_b, g_ffn_b)
    g_ffo_bias = jnp.sum(g_ffn_b.astype(jnp.float32), 0)
    g_act = dot_second(g_ffn_b, ffo_back)
    gelu_value, gelu_pull = jax.vjp(gelu_exact, hidden)
    g_hidden_b = gelu_pull(g_act)[0].astype(jnp.bfloat16)
    g_in = dot_first(first_b, g_hidden_b)
    g_in_bias = jnp.sum(g_hidden_b.astype(jnp.float32), 0)
    g_first = g_resid_two + dot_second(g_hidden_b, in_back)
    norm_one, norm_one_pull = jax.vjp(layer_norm, resid_one, norm_gains[0], layer_biases[4])
    g_resid_one, g_gain_one, g_shift_one = norm_one_pull(g_first)
    g_branch_b = g_resid_one.astype(jnp.bfloat16)
    g_outw = dot_first(att_b, g_branch_b)
    g_out_bias = jnp.sum(g_branch_b.astype(jnp.float32), 0)
    g_att_b = dot_second(g_branch_b, out_back).astype(jnp.bfloat16)
    g_query_rows, g_keys_all, g_values_all = attend_backward(
        queries, keys_all, values_all, allowed, g_att_b, log_totals
    )
    query_grad_b = g_query_rows.astype(jnp.bfloat16)
    cont_kv_b = jnp.concatenate([g_keys_all[prompt_len:], g_values_all[prompt_len:]], 1).astype(
        jnp.bfloat16
    )
    block_kv_b = jnp.concatenate([g_keys_all[:prompt_len], g_values_all[:prompt_len]], 1).astype(
        jnp.bfloat16
    )
    kv_weights = qkv_back[:, D:]
    g_query_w = dot_first(tokens, query_grad_b)
    g_kv_w = dot_first(tokens[prompt_rows:], cont_kv_b)
    g_tokens = g_resid_one + dot_second(query_grad_b, qkv_back[:, :D])
    cont_through = dot_second(cont_kv_b, kv_weights)
    kv_summed = lax.psum_scatter(
        block_kv_b.astype(jnp.float32).astype(jnp.bfloat16),
        "shard",
        scatter_dimension=0,
        tiled=True,
    ).astype(jnp.float32)
    g_kv_w = g_kv_w + lax.dot_general(
        tokens_f[:prompt_rows],
        kv_summed,
        (((0,), (0,)), ((), ())),
        precision=HIGHEST,
        preferred_element_type=jnp.float32,
    )
    prompt_through = jnp.dot(
        kv_summed,
        kv_weights.astype(jnp.float32).T,
        precision=HIGHEST,
        preferred_element_type=jnp.float32,
    )
    value_cols = jnp.sum(kv_summed[:, D:], 0)
    g_tokens = g_tokens + jnp.concatenate([prompt_through, cont_through], 0)
    g_qkvw = jnp.concatenate([g_query_w, g_kv_w], 1)
    g_query_bias = jnp.sum(query_grad_b.astype(jnp.float32), 0)
    g_value_bias = jnp.sum(cont_kv_b[:, D:].astype(jnp.float32), 0) + value_cols
    owned = (
        lax.psum_scatter(
            g_qkvw.astype(jnp.bfloat16), "shard", scatter_dimension=0, tiled=True
        ).astype(jnp.float32),
        lax.psum_scatter(
            g_outw.astype(jnp.bfloat16), "shard", scatter_dimension=0, tiled=True
        ).astype(jnp.float32),
        lax.psum_scatter(
            g_in.astype(jnp.bfloat16), "shard", scatter_dimension=0, tiled=True
        ).astype(jnp.float32),
        lax.psum_scatter(
            g_ffo.astype(jnp.bfloat16), "shard", scatter_dimension=0, tiled=True
        ).astype(jnp.float32),
    )
    owned_qkv, owned_out, owned_in, owned_ffo = (
        lax.psum(owned[0].astype(jnp.bfloat16), "rep").astype(jnp.float32),
        lax.psum(owned[1].astype(jnp.bfloat16), "rep").astype(jnp.float32),
        lax.psum(owned[2].astype(jnp.bfloat16), "rep").astype(jnp.float32),
        lax.psum(owned[3].astype(jnp.bfloat16), "rep").astype(jnp.float32),
    )
    g_biases = jnp.stack(
        [g_query_bias, g_value_bias, g_out_bias, g_ffo_bias, g_shift_one, g_shift_two]
    )
    g_gains = jnp.stack([g_gain_one, g_gain_two])
    g_vectors = jnp.stack([g_sbias, g_query, g_pbias])
    summed = lax.psum(
        (g_biases, g_gains, g_in_bias, g_student, g_vectors, g_pool, g_class, g_cbias),
        ("rep", "shard"),
    )
    return (
        output_b[:prompt_rows][None],
        output_b[prompt_rows:][None, None],
        logit_row[None, None],
        g_tokens[:prompt_rows][None],
        g_tokens[prompt_rows:][None, None],
        owned_qkv,
        owned_out,
        owned_in,
        owned_ffo,
        summed[0],
        summed[1],
        summed[2],
        summed[3],
        summed[4],
        summed[5],
        summed[6],
        summed[7],
    )


def solution(mesh):
    return jax.shard_map(
        body,
        mesh=mesh,
        in_specs=(
            P("rep", "shard", None),
            P("rep", "shard", None, None),
            P("rep", "shard", None),
            P("rep", "shard", None, None),
            P("rep", "shard"),
            P("shard", None),
            P("shard", None),
            P("shard", None),
            P("shard", None),
            P(),
            P(),
            P(),
            P(),
            P(),
            P(),
            P(),
            P(),
        ),
        out_specs=(
            P("rep", "shard", None),
            P("rep", "shard", None, None),
            P("rep", "shard", None),
            P("rep", "shard", None),
            P("rep", "shard", None, None),
            P("shard", None),
            P("shard", None),
            P("shard", None),
            P("shard", None),
            P(),
            P(),
            P(),
            P(),
            P(),
            P(),
            P(),
            P(),
        ),
        check_vma=False,
    )
```

profile of v0, /device:TPU:1, one launch (start us, length us, event | category | flops | bytes accessed | tf_op | source)
XLA Modules:
  0.0 1007.4 jit_solution(7969806802003201834)
XLA Ops:
  7.3 2.6 convert_element_type.145
  10.5 32.9 %all-gather.7.cloned.1.call-done = bf16[768,2304]{1,0:T(8,128)(2,1)} async-done(((bf16[192,2304]{1,0:T(8,128)(2,1)}), bf16[768,2304]{1,0:T(8,128)(2,1)}) %all-gather.7.cloned.1.call-update) | async-done | bytes 3538960 | tf_op jit(solution)/shard_map/all_gather | solution.py:140
  43.4 5.3 add_convert_fusion.1
  54.4 2.9 convert_element_type.154
  60.1 2.6 fusion.99
  65.1 6.2 all-gather.11.cloned.1.call-done
  73.1 20.0 %all-gather.9.cloned.1.call-done = bf16[1024,768]{1,0:T(8,128)(2,1)} async-done(((bf16[256,768]{1,0:T(8,128)(2,1)}), bf16[1024,768]{1,0:T(8,128)(2,1)}) %all-gather.9.cloned.1.call-update) | async-done | bytes 1572880 | tf_op jit(solution)/shard_map/all_gather | solution.py:154
  93.1 3.2 pad_maximum_fusion.2
  97.4 133.8 %while.28 = (s32[]{:T(128)}, bf16[12,768,64]{1,2,0:T(8,128)(2,1)}, f32[12,768]{1,0:T(8,128)}, s32[12]{0:T(128)S(1)}, bf16[768,768]{1,0:T(8,128)(2,1)}, /*index=5...) while((s32[]{:T(128)}, bf16[12,768,64]{1,2,0:T(8,128)(2,1)}, ...), condition=%wide.region_3.4_spmd.clone, body=%wide.region_0.3_spmd.clone.sunk | while | flops 312605952 | bytes 34253524 | solution.py:66
  104.4 4.1 fusion.160
  115.5 4.1 fusion.160
  126.7 4.1 fusion.160
  137.8 4.1 fusion.160
  148.9 4.2 fusion.160
  160.0 4.6 fusion.160
  171.6 4.1 fusion.160
  182.6 4.2 fusion.160
  193.8 4.1 fusion.160
  204.9 4.1 fusion.160
  216.0 4.1 fusion.160
  227.1 4.1 fusion.160
  232.6 3.1 fusion.100
  236.5 29.4 %multiply_convert_fusion.1 = (bf16[768,3072]{1,0:T(8,128)(2,1)}, f32[768,3072]{1,0:T(8,128)}, f32[768,3072]{1,0:T(8,128)}) fusion(f32[3072]{0:T(1024)S(1)} %copy-done.42, bf16[768,3072]{1,0:T(8,128)(2,1)} %all-gather.15.cloned.1.call-done, f32[768,768]{0,1:T(8,128)S(1)} %get-tuple-element.319, f32[768]{0:T(1024)S(1)} %get-tuple-element.226, ...), kind=kOutput, calls=%fused_computation.48 | convolution fusion | flops 3782541312 | bytes 30695424 | tf_op jit(solution)/shard_map/dot_general | solution.py:18
  266.0 8.7 fusion.101
  294.1 13.0 %convert_reduce_fusion = (f32[3072]{0:T(1024)S(1)}, bf16[768,3072]{1,0:T(8,128)(2,1)S(1)}) fusion(f32[768,3072]{1,0:T(8,128)} %get-tuple-element.302, f32[768,3072]{1,0:T(8,128)} %get-tuple-element.320, f32[3072]{0:T(1024)S(1)} %copy-done.43, bf16[768,768]{0,1:T(8,128)(2,1)S(1)} %get-tuple-element.288, bf16[3072,768]{1,0:T(8,128)(2,1)} %all-gather.17.cloned.1.call-done), kind=kOutput, calls=%fused_computation.46 | convolution fusion | flops 3663983616 | bytes 29515776 | tf_op jit(solution)/shard_map/dot_general | solution.py:28
  307.2 4.5 multiply_reduce_fusion.2
  317.1 168.6 %while.29 = (s32[]{:T(128)}, bf16[12,768,64]{1,2,0:T(8,128)(2,1)}, bf16[12,1536,64]{1,2,0:T(8,128)(2,1)}, bf16[12,1536,64]{1,2,0:T(8,128)(2,1)}, s32[12]{0:T(128...) while((s32[]{:T(128)}, bf16[12,768,64]{1,2,0:T(8,128)(2,1)}, ...), condition=%wide.region_23.24_spmd.clone, body=%wide.region_21.23_spmd.clone.sunk | while | flops 766917888 | bytes 38360792 | solution.py:88
  326.4 2.5 fusion.169
  354.4 2.5 fusion.169
  368.5 2.5 fusion.169
  382.5 2.5 fusion.169
  396.6 2.5 fusion.169
  424.7 2.5 fusion.169
  480.9 2.5 fusion.169
  496.7 31.8 %reduce-scatter.8.cloned.1.call-done = bf16[256,1536]{0,1:T(8,128)(2,1)} async-done(((bf16[1024,1536]{0,1:T(8,128)(2,1)}), bf16[256,1536]{0,1:T(8,128)(2,1)}) %reduce-scatter.8.cloned.1.call-update) | async-done | bytes 786448 | tf_op jit(solution)/shard_map/reduce_scatter | solution.py:245
  534.0 5.8 copy.89
  539.9 3.8 convolution_convert_fusion.2
  543.8 9.7 convolution_convert_fusion.1
  553.5 8.8 convolution_convert_fusion
  562.4 18.0 %reduce-scatter.16.cloned.1.call-done = bf16[192,2304]{1,0:T(8,128)(2,1)} async-done(((bf16[768,2304]{1,0:T(8,128)(2,1)}), bf16[192,2304]{1,0:T(8,128)(2,1)}) %reduce-scatter.16.cloned.1.call-update) | async-done | bytes 884752
  582.7 26.4 %reduce-scatter.10.cloned.1.call-done = bf16[192,768]{1,0:T(8,128)(2,1)} async-done(((bf16[768,768]{1,0:T(8,128)(2,1)}), bf16[192,768]{1,0:T(8,128)(2,1)}) %reduce-scatter.10.cloned.1.call-update) | async-done | bytes 294928 | tf_op jit(solution)/shard_map/reduce_scatter | solution.py:273
  609.2 50.4 %reduce-scatter.12.cloned.1.call-done = bf16[192,3072]{1,0:T(8,128)(2,1)} async-done(((bf16[768,3072]{1,0:T(8,128)(2,1)}), bf16[192,3072]{1,0:T(8,128)(2,1)}) %reduce-scatter.12.cloned.1.call-update) | async-done | bytes 1179664 | tf_op jit(solution)/shard_map/reduce_scatter | solution.py:276
  659.6 50.5 %reduce-scatter.14.cloned.1.call-done = bf16[768,768]{1,0:T(8,128)(2,1)} async-done(((bf16[3072,768]{1,0:T(8,128)(2,1)}), bf16[768,768]{1,0:T(8,128)(2,1)}) %reduce-scatter.14.cloned.1.call-update) | async-done | bytes 1179664 | tf_op jit(solution)/shard_map/reduce_scatter | solution.py:279
  724.0 3.4 fusion.47
  735.8 43.7 %all-reduce.1 = (f32[6,768]{1,0:T(8,128)}, f32[2,768]{1,0:T(2,128)}, f32[3072]{0:T(1024)}, f32[3,128]{1,0:T(4,128)}, f32[128,14]{0,1:T(8,128)}, /*index=5*/f32[14]{0:T(128)}) all-reduce(f32[6,768]{1,0:T(8,128)S(1)} %stack.32, f32[2,768]{1,0:T(2,128)S(1)} %pad_maximum_fusion.11, ...), channel_id=1, replica_groups=mesh['rep'=8,'shard'=4] {'rep','shard'}, use_global_device_ids=true, to_apply=%region_40.41 | all-reduce | flops 11406 | bytes 91248 | tf_op jit(solution)/shard_map/psum | solution.py:294
  779.4 83.9 %all-reduce.9.cloned.1.call-done = (bf16[192,2304]{0,1:T(8,128)(2,1)}, bf16[192,768]{1,0:T(8,128)(2,1)}, bf16[192,3072]{1,0:T(8,128)(2,1)}, bf16[768,768]{1,0:T(8,128)(2,1)}) async-done(((bf16[192,2304]{0,1:T(8,128)(2,1)}, bf16[192,768]{1,0:T(8,128)(2,1)}, bf16[192,3072]{1,0:T(8,128)(2,1)}, bf16[768,768]{1,0:T(8,128)(2,1)}), (bf16[192,2304]{0,1:T(8,128)(2,1)}, bf16[192,768]{1,0:T(8,128)(2,1)}, ...) | async-done | bytes 3538960 | tf_op jit(solution)/shard_map/psum | solution.py:284
  863.4 3.0 convert_element_type.173
  870.5 126.7 %all-reduce.7.cloned.1.call-done = (f32[768,128]{1,0:T(8,128)}, f32[128,128]{1,0:T(8,128)}) async-done(((f32[768,128]{1,0:T(8,128)}, f32[128,128]{1,0:T(8,128)}), (f32[768,128]{1,0:T(8,128)}, f32[128,128]{1,0:T(8,128)})) %all-reduce.7.cloned.1.call-update) | async-done | bytes 458768 | tf_op jit(solution)/shard_map/psum | solution.py:294
  (423 shorter events, 305.3 us)
Async XLA Ops:
  7.2 271.6 %copy-start = (f32[128,128]{1,0:T(8,128)S(1)}, f32[128,128]{1,0:T(8,128)}, u32[]{:S(2)}) copy-start(f32[128,128]{1,0:T(8,128)} %param.35) | copy-start | bytes 196612
  7.2 2.7 copy-start.13
  7.2 3.0 copy-start.17
  7.2 3.2 copy-start.36
  7.2 36.2 %all-gather.7.cloned.1.call-start = ((), (), s32[]{:S(2)}) async-start(), calls=%async_computation.5 | async-start | bytes 4423680 | tf_op jit(solution)/shard_map/all_gather | solution.py:140
  9.9 61.4 %all-gather.11.cloned.1.call-start = ((), (), s32[]{:S(2)}) async-start(), calls=%async_computation.7 | async-start | bytes 1966080 | tf_op jit(solution)/shard_map/all_gather | solution.py:155
  10.2 33.2 %copy-start.27 = (bf16[1,1,512,768]{2,3,1,0:T(8,128)(2,1)}, bf16[1,1,512,768]{2,3,1,0:T(8,128)(2,1)S(1)}, u32[]{:S(2)}) copy-start(bf16[1,1,512,768]{2,3,1,0:T(8,128)(2,1)S(1)} %copy.63) | copy-start | bytes 2359300
  10.4 33.0 %copy-start.31 = (bf16[1,256,768]{1,2,0:T(8,128)(2,1)}, bf16[1,256,768]{1,2,0:T(8,128)(2,1)S(1)}, u32[]{:S(2)}) copy-start(bf16[1,256,768]{1,2,0:T(8,128)(2,1)S(1)} %copy.62) | copy-start | bytes 1179652
  43.4 8.8 copy-start.29
  50.5 2.6 copy-start.16
  51.5 41.6 %all-gather.9.cloned.1.call-start = ((), (), s32[]{:S(2)}) async-start(), calls=%async_computation.6 | async-start | bytes 1966080 | tf_op jit(solution)/shard_map/all_gather | solution.py:154
  52.2 179.0 %all-gather.13.cloned.1.call-start = ((), (), s32[]{:S(2)}) async-start(), calls=%async_computation.8 | async-start | bytes 1474560 | tf_op jit(solution)/shard_map/all_gather | solution.py:141
  53.0 183.1 %all-gather.15.cloned.1.call-start = ((), (), s32[]{:S(2)}) async-start(), calls=%async_computation.9 | async-start | bytes 5898240 | tf_op jit(solution)/shard_map/all_gather | solution.py:142
  54.3 3.1 copy-start.37
  54.3 3.1 copy-start.38
  54.3 4.5 copy-start.26
  54.3 4.8 copy-start.30
  54.3 211.6 %all-gather.17.cloned.1.call-start = ((), (), s32[]{:S(2)}) async-start(), calls=%async_computation.10 | async-start | bytes 5898240 | tf_op jit(solution)/shard_map/all_gather | solution.py:143
  57.3 471.2 %reduce-scatter.8.cloned.1.call-start = ((), (), s32[]{:S(2)}) async-start(), calls=%async_computation.11 | async-start | bytes 3932160 | tf_op jit(solution)/shard_map/reduce_scatter | solution.py:245
  123.1 2.2 copy-start.2
  134.3 2.1 copy-start.2
  235.8 30.1 %copy-start.6 = (f32[768,768]{0,1:T(8,128)}, f32[768,768]{0,1:T(8,128)S(1)}, u32[]{:S(2)}) copy-start(f32[768,768]{0,1:T(8,128)S(1)} %get-tuple-element.319) | copy-start | bytes 7077892
  274.9 4.0 copy-start.35
  280.4 4.5 copy-start.39
  287.3 4.3 copy-start.11
  290.2 2.5 copy-start.23
  293.4 13.7 %slice-start = ((s8[4718592]{0:T(1024)(128)(4,1)}), s8[4194304]{0:T(1024)(128)(4,1)S(1)}, s32[]{:S(2)}) async-start(s8[4718592]{0:T(1024)(128)(4,1)} %bitcast.224), calls=%async_computation.18 | async-start | bytes 8388608
  293.7 13.4 %copy-start.19 = (bf16[768,768]{0,1:T(8,128)(2,1)}, bf16[768,768]{0,1:T(8,128)(2,1)S(1)}, u32[]{:S(2)}) copy-start(bf16[768,768]{0,1:T(8,128)(2,1)S(1)} %get-tuple-element.288) | copy-start | bytes 3538948
  294.1 13.0 %copy-start.7 = (f32[768,768]{0,1:T(8,128)S(1)}, f32[768,768]{0,1:T(8,128)}, u32[]{:S(2)}) copy-start(f32[768,768]{0,1:T(8,128)} %copy-done.6) | copy-start | bytes 7077892
  294.1 13.1 %slice-start.1 = ((s8[4718592]{0:T(1024)(128)(4,1)}), s8[524288]{0:T(1024)(128)(4,1)S(1)}, s32[]{:S(2)}) async-start(s8[4718592]{0:T(1024)(128)(4,1)} %bitcast.224), calls=%async_computation.19 | async-start | bytes 1048576
  307.2 4.6 copy-start.44
  312.7 3.3 copy-start.20
  490.9 89.5 %reduce-scatter.16.cloned.1.call-start = ((), (), s32[]{:S(2)}) async-start(), calls=%async_computation.15 | async-start | bytes 4423680
  491.1 3.5 copy-start.4
  491.1 3.5 copy-start.28
  491.2 3.4 copy-start.32
  528.5 2.1 copy-start.14
  528.5 2.1 copy-start.15
  539.9 69.3 %reduce-scatter.10.cloned.1.call-start = ((), (), s32[]{:S(2)}) async-start(), calls=%async_computation.12 | async-start | bytes 1474560 | tf_op jit(solution)/shard_map/reduce_scatter | solution.py:273
  543.7 115.9 %reduce-scatter.12.cloned.1.call-start = ((), (), s32[]{:S(2)}) async-start(), calls=%async_computation.13 | async-start | bytes 5898240 | tf_op jit(solution)/shard_map/reduce_scatter | solution.py:276
  553.5 156.6 %reduce-scatter.14.cloned.1.call-start = ((), (), s32[]{:S(2)}) async-start(), calls=%async_computation.14 | async-start | bytes 5898240 | tf_op jit(solution)/shard_map/reduce_scatter | solution.py:279
  562.3 301.0 %all-reduce.9.cloned.1.call-start = ((), (), s32[]{:S(2)}) async-start(), calls=%async_computation.17 | async-start | bytes 7667712 | tf_op jit(solution)/shard_map/psum | solution.py:284
  710.1 287.0 %all-reduce.7.cloned.1.call-start = ((), (), s32[]{:S(2)}) async-start(), calls=%async_computation.16 | async-start | bytes 917504 | tf_op jit(solution)/shard_map/psum | solution.py:294
  714.7 7.0 copy-start.24
  724.0 3.4 copy-start.10
  724.0 3.6 copy-start.33
  863.4 3.0 copy-start.21
  868.0 132.4 %copy-start.1 = (f32[128,128]{1,0:T(8,128)S(1)}, f32[128,128]{1,0:T(8,128)}, u32[]{:S(2)}) copy-start(f32[128,128]{1,0:T(8,128)} %param.35) | copy-start | bytes 196612
  (23 other events, 37.7 us)
Sparse Core Ops, SparseCore 0:
  10.2 33.1 all-gather.6
  51.6 19.6 all-gather.10
  73.4 19.6 all-gather.8
  95.1 17.4 all-gather.12
  114.5 37.4 all-gather.14
  153.4 37.4 all-gather.16
  491.0 37.4 reduce-scatter.7
  540.0 40.3 reduce-scatter.15
  583.6 25.5 reduce-scatter.9
  611.6 47.9 reduce-scatter.11
  662.1 47.9 reduce-scatter.13
  714.6 148.7 all-reduce.8
  869.3 127.8 all-reduce.6
where the time goes:
time: 1020 us; the launch traced here: 1010 us
  waiting for transfers between devices  448 us (44%)
  matrix products  322 us (32%)
  local copies, waits for them, and re-layouts  108 us (11%)
  other arithmetic  50.7 us (5%)
  blocking collectives  43.7 us (4%)
  between operations  17.9 us (2%)
  loops' own time  16.2 us (2%)
    dot_general x29, matrix products, dot_plain(): return jnp.dot(left, right, preferred_element_type=jnp.float32)  127 us
    psum x1, waiting for transfers between devices, body(): lax.psum((g_biases, g_gains, g_in_bias, g_student, g_vectors, g_pool, g_c...  127 us
    dot_general x42, matrix products, dot_second(): lax.dot_general(left, right, (((1,), (1,)), ((), ())), preferred_element_...  107 us
    psum x1, waiting for transfers between devices, body(): lax.psum(owned[0].astype(jnp.bfloat16), 'rep').astype(jnp.float32)  83.9 us
    dot_general x30, matrix products, dot_first(): lax.dot_general(left, right, (((0,), (0,)), ((), ())), preferred_element_...  82.1 us
    reduce_scatter x1, waiting for transfers between devices, body(): lax.psum_scatter(g_ffo.astype(jnp.bfloat16), 'shard', scatter_dimension=0...  50.5 us
    reduce_scatter x1, waiting for transfers between devices, body(): lax.psum_scatter(g_in.astype(jnp.bfloat16), 'shard', scatter_dimension=0,...  50.4 us
    psum x1, blocking collectives, body(): lax.psum((g_biases, g_gains, g_in_bias, g_student, g_vectors, g_pool, g_c...  43.7 us
  transfers between devices with their start and end apart: 13, of which 10 were waited for; matrix products, arithmetic and copies ran while one was open for 22% of the time, Pallas kernels for 0%

commit v1 on v0

--- a/solution.py
+++ b/solution.py
@@ -1,6 +1,10 @@
+from functools import partial
+
 import jax
 import jax.numpy as jnp
 from jax import lax
+from jax.experimental import pallas as pl
+from jax.experimental.pallas import tpu as pltpu
 from jax.sharding import PartitionSpec as P
 
 D = 768
@@ -12,6 +16,7 @@
 
 HIGHEST = lax.Precision.HIGHEST
 NEG_BIG = -1e30
+ATTN_VMEM = 48 * 1024 * 1024
 
 
 def dot_plain(left, right):
@@ -28,10 +33,6 @@
     return lax.dot_general(
         left, right, (((1,), (1,)), ((), ())), preferred_element_type=jnp.float32
     )
-
-
-def column_slice(matrix, head_index):
-    return lax.dynamic_slice_in_dim(matrix, head_index * DH, DH, 1)
 
 
 def layer_norm(values, gain, shift):
@@ -44,53 +45,246 @@
     return jax.nn.gelu(values, approximate=False)
 
 
-def attend_forward(queries, keys_all, values_all, allowed):
+def aug_parts(values):
+    high = values.astype(jnp.bfloat16).astype(jnp.float32)
+    rest = values - high
+    mid = rest.astype(jnp.bfloat16).astype(jnp.float32)
+    return (high, mid, rest - mid)
+
+
+def attend_forward_kernel(prompt_rows, prompt_len, q_ref, kp_ref, vp_ref, k_ref, v_ref, o_ref, lse_ref):
+    half = (q_ref.shape[0] - prompt_rows) // 2
+    mid = prompt_rows + half
+    start = lax.axis_index("shard") * prompt_rows
+    width = 2 * DH
+    chunk = min(512, prompt_len)
+    outs = []
+    logs = []
+    for head in range(2):
+        def lane_mask(rows):
+            lane = lax.broadcasted_iota(jnp.int32, (rows, width), 1)
+            return (lane >= DH) if head else (lane < DH)
+
+        def attend(queries, segments):
+            rows = queries.shape[0]
+            scaled = jnp.where(lane_mask(rows), queries * jnp.bfloat16(DH ** (-0.5)), jnp.bfloat16(0))
+            scores = []
+            largest = None
+            for keys, values, mask in segments:
+                part = dot_second(scaled, keys)
+                if mask is not None:
+                    part = jnp.where(mask, part, NEG_BIG)
+                scores.append(part)
+                top = jnp.max(part, 1, keepdims=True)
+                largest = top if largest is None else jnp.maximum(largest, top)
+            total = None
+            for part, (keys, values, mask) in zip(scores, segments):
+                probs = jnp.exp(part - largest).astype(jnp.bfloat16)
+                ones = jnp.ones(values.shape, jnp.bfloat16)
+                both = dot_plain(probs, jnp.concatenate([values, ones], 1))
+                total = both if total is None else total + both
+            norm = total[:, width:]
+            return (total[:, :width] / norm, largest + jnp.log(norm))
+
+        def prompt_segments(masked):
+            found = []
+            for at in range(0, prompt_len, chunk):
+                mask = None
+                if masked:
+                    query = lax.broadcasted_iota(jnp.int32, (prompt_rows, chunk), 0) + start
+                    key = lax.broadcasted_iota(jnp.int32, (prompt_rows, chunk), 1) + at
+                    mask = key <= query
+                found.append((kp_ref[at : at + chunk, :], vp_ref[at : at + chunk, :], mask))
+            return found
+
+        def causal(size):
+            return lax.broadcasted_iota(jnp.int32, (size, size), 1) <= lax.broadcasted_iota(
+                jnp.int32, (size, size), 0
+            )
+
+        first = (k_ref[prompt_rows:mid, :], v_ref[prompt_rows:mid, :])
+        second = (k_ref[mid:, :], v_ref[mid:, :])
+        pieces = [
+            attend(q_ref[:prompt_rows, :], prompt_segments(True)),
+            attend(q_ref[prompt_rows:mid, :], prompt_segments(False) + [first + (causal(half),)]),
+            attend(
+                q_ref[mid:, :],
+                prompt_segments(False) + [first + (None,), second + (causal(half),)],
+            ),
+        ]
+        outs.append(jnp.concatenate([piece[0] for piece in pieces], 0))
+        logs.append(jnp.concatenate([piece[1] for piece in pieces], 0))
+    left = lax.broadcasted_iota(jnp.int32, outs[0].shape, 1) < DH
+    o_ref[...] = jnp.where(left, outs[0], outs[1]).astype(o_ref.dtype)
+    lse_ref[...] = jnp.where(left, logs[0], logs[1])
+
+
+def attend_forward(qkv_b, kv_prompt):
+    rows = qkv_b.shape[0]
+    prompt_len = kv_prompt.shape[0]
+    prompt_rows = prompt_len // lax.axis_size("shard")
+    cont_len = rows - prompt_rows
+    width = 2 * DH
+    pairs = D // width
+    return pl.pallas_call(
+        partial(attend_forward_kernel, prompt_rows, prompt_len),
+        grid=(pairs,),
+        in_specs=[
+            pl.BlockSpec((rows, width), lambda pair: (0, pair)),
+            pl.BlockSpec((prompt_len, width), lambda pair: (0, pair)),
+            pl.BlockSpec((prompt_len, width), lambda pair: (0, pairs + pair)),
+            pl.BlockSpec((rows, width), lambda pair: (0, pairs + pair)),
+            pl.BlockSpec((rows, width), lambda pair: (0, 2 * pairs + pair)),
+        ],
+        out_specs=[
+            pl.BlockSpec((rows, width), lambda pair: (0, pair)),
+            pl.BlockSpec((rows, width), lambda pair: (0, pair)),
+        ],
+        out_shape=[
+            jax.ShapeDtypeStruct((rows, D), jnp.bfloat16),
+            jax.ShapeDtypeStruct((rows, D), jnp.float32),
+        ],
+        compiler_params=pltpu.CompilerParams(vmem_limit_bytes=ATTN_VMEM),
+        name="attend_forward",
+    )(qkv_b, kv_prompt, kv_prompt, qkv_b, qkv_b)
+
+
+def attend_backward_kernel(
+    prompt_rows, prompt_len, q_ref, kp_ref, vp_ref, k_ref, v_ref, o_ref, go_ref, lse_ref,
+    gq_ref, gkp_ref, gvp_ref, gkc_ref, gvc_ref, acc_ref
+):
+    rows = q_ref.shape[0]
+    cont_len = rows - prompt_rows
+    half = cont_len // 2
+    mid = prompt_rows + half
+    start = lax.axis_index("shard") * prompt_rows
+    width = 2 * DH
     scaling = DH ** (-0.5)
-
-    def one_head(head_index):
-        scores = jnp.where(
-            allowed,
-            dot_second(column_slice(queries, head_index), column_slice(keys_all, head_index))
-            * scaling,
-            NEG_BIG,
+    low = jnp.bfloat16
+    prods = o_ref[...].astype(jnp.float32) * go_ref[...].astype(jnp.float32)
+    lane = lax.broadcasted_iota(jnp.int32, (rows, width), 1)
+    left = lane < DH
+    augmented = []
+    for head in range(2):
+        own = jnp.logical_not(left) if head else left
+        at = 0 if head else DH
+        delta = jnp.sum(jnp.where(own, prods, 0.0), 1, keepdims=True)
+        log_total = lse_ref[:, head * DH : head * DH + 1]
+
+        def extend(values, shift):
+            high, middle, rest = aug_parts(-shift)
+            extra = jnp.where(
+                lane == at, high, jnp.where(lane == at + 1, middle, jnp.where(lane == at + 2, rest, 0.0))
+            ).astype(low)
+            return jnp.where(own, values, extra)
+
+        augmented.append(
+            (extend(q_ref[...] * low(scaling), log_total), extend(go_ref[...], delta))
         )
-        largest = jnp.max(scores, 1, keepdims=True)
-        expo = jnp.exp(scores - largest)
-        total = jnp.sum(expo, 1, keepdims=True)
-        probs = (expo / total).astype(jnp.bfloat16)
+    acc_ref[...] = jnp.zeros_like(acc_ref)
+
+    def one_block(keys, values, spans):
+        size = keys.shape[0]
+        key_lane = lax.broadcasted_iota(jnp.int32, (size, width), 1)
+        key_left = key_lane < DH
+        grads_k = []
+        grads_v = []
+        for head in range(2):
+            at = 0 if head else DH
+            ones = jnp.logical_and(key_lane >= at, key_lane < at + 3)
+            own = jnp.logical_not(key_left) if head else key_left
+
+            def extend(block):
+                return jnp.where(own, block, jnp.where(ones, low(1), low(0)))
+
+            keys_x, values_x = extend(keys), extend(values)
+            q_x, go_x = augmented[head]
+            grad_k = None
+            grad_v = None
+            for lo, hi, mask in spans:
+                scores = dot_second(keys_x, q_x[lo:hi])
+                if mask is not None:
+                    scores = jnp.where(mask, scores, NEG_BIG)
+                probs = jnp.exp(scores)
+                g_scores = (probs * dot_second(values_x, go_x[lo:hi])).astype(low)
+                part_v = dot_plain(probs.astype(low), go_ref[lo:hi, :])
+                part_k = dot_plain(g_scores, q_ref[lo:hi, :])
+                grad_k = part_k if grad_k is None else grad_k + part_k
+                grad_v = part_v if grad_v is None else grad_v + part_v
+                acc_ref[head, lo:hi, :] += dot_first(g_scores, keys)
+            grads_k.append(grad_k)
+            grads_v.append(grad_v)
         return (
-            dot_plain(probs, column_slice(values_all, head_index)),
-            (largest + jnp.log(total))[:, 0],
+            jnp.where(key_left, grads_k[0], grads_k[1]) * scaling,
+            jnp.where(key_left, grads_v[0], grads_v[1]),
         )
 
-    heads, log_totals = lax.map(one_head, jnp.arange(HEADS))
-    return (heads.transpose(1, 0, 2).reshape(queries.shape[0], HEADS * DH), log_totals)
-
-
-def attend_backward(queries, keys_all, values_all, allowed, grad_att, log_totals):
-    scaling = DH ** (-0.5)
-
-    def one_head(item):
-        head_index, log_row = item
-        query_h = column_slice(queries, head_index)
-        key_h = column_slice(keys_all, head_index)
-        grad_h = column_slice(grad_att, head_index)
-        scores = jnp.where(allowed, dot_second(query_h, key_h) * scaling, NEG_BIG)
-        probs = jnp.exp(scores - log_row[:, None])
-        grad_probs = dot_second(grad_h, column_slice(values_all, head_index))
-        delta = jnp.sum(grad_probs * probs, 1, keepdims=True)
-        grad_scores = (probs * (grad_probs - delta)).astype(jnp.bfloat16)
-        grad_query = dot_plain(grad_scores, key_h) * scaling
-        grad_key = dot_first(grad_scores, query_h) * scaling
-        grad_value = dot_first(probs.astype(jnp.bfloat16), grad_h)
-        return (grad_query, grad_key, grad_value)
-
-    grad_q, grad_k, grad_v = lax.map(one_head, (jnp.arange(HEADS), log_totals))
-
-    def merge_heads(block):
-        return block.transpose(1, 0, 2).reshape(block.shape[1], HEADS * DH)
-
-    return (merge_heads(grad_q), merge_heads(grad_k), merge_heads(grad_v))
+    chunk = prompt_rows
+
+    def prompt_block(index, carry):
+        at = pl.multiple_of(index * chunk, chunk)
+        key = lax.broadcasted_iota(jnp.int32, (chunk, prompt_rows), 0) + at
+        query = lax.broadcasted_iota(jnp.int32, (chunk, prompt_rows), 1) + start
+        grad_k, grad_v = one_block(
+            kp_ref[pl.ds(at, chunk), :],
+            vp_ref[pl.ds(at, chunk), :],
+            [(0, prompt_rows, key <= query), (prompt_rows, rows, None)],
+        )
+        gkp_ref[pl.ds(at, chunk), :] = grad_k.astype(low)
+        gvp_ref[pl.ds(at, chunk), :] = grad_v.astype(low)
+        return carry
+
+    lax.fori_loop(0, prompt_len // chunk, prompt_block, 0)
+    causal = lax.broadcasted_iota(jnp.int32, (half, half), 0) <= lax.broadcasted_iota(
+        jnp.int32, (half, half), 1
+    )
+    grad_k, grad_v = one_block(
+        k_ref[prompt_rows:mid, :], v_ref[prompt_rows:mid, :], [(prompt_rows, mid, causal), (mid, rows, None)]
+    )
+    gkc_ref[:half, :] = grad_k.astype(low)
+    gvc_ref[:half, :] = grad_v.astype(low)
+    grad_k, grad_v = one_block(k_ref[mid:, :], v_ref[mid:, :], [(mid, rows, causal)])
+    gkc_ref[half:, :] = grad_k.astype(low)
+    gvc_ref[half:, :] = grad_v.astype(low)
+    gq_ref[...] = (jnp.where(left, acc_ref[0], acc_ref[1]) * scaling).astype(low)
+
+
+def attend_backward(qkv_b, kv_prompt, att_b, grad_att, log_totals):
+    rows = qkv_b.shape[0]
+    prompt_len = kv_prompt.shape[0]
+    prompt_rows = prompt_len // lax.axis_size("shard")
+    cont_len = rows - prompt_rows
+    width = 2 * DH
+    pairs = D // width
+
+    def column(count):
+        return pl.BlockSpec((count, width), lambda pair: (0, pair))
+
+    return pl.pallas_call(
+        partial(attend_backward_kernel, prompt_rows, prompt_len),
+        grid=(pairs,),
+        in_specs=[
+            column(rows),
+            column(prompt_len),
+            pl.BlockSpec((prompt_len, width), lambda pair: (0, pairs + pair)),
+            pl.BlockSpec((rows, width), lambda pair: (0, pairs + pair)),
+            pl.BlockSpec((rows, width), lambda pair: (0, 2 * pairs + pair)),
+            column(rows),
+            column(rows),
+            column(rows),
+        ],
+        out_specs=[column(rows), column(prompt_len), column(prompt_len), column(cont_len), column(cont_len)],
+        out_shape=[
+            jax.ShapeDtypeStruct((rows, D), jnp.bfloat16),
+            jax.ShapeDtypeStruct((prompt_len, D), jnp.bfloat16),
+            jax.ShapeDtypeStruct((prompt_len, D), jnp.bfloat16),
+            jax.ShapeDtypeStruct((cont_len, D), jnp.bfloat16),
+            jax.ShapeDtypeStruct((cont_len, D), jnp.bfloat16),
+        ],
+        scratch_shapes=[pltpu.VMEM((2, rows, width), jnp.float32)],
+        compiler_params=pltpu.CompilerParams(vmem_limit_bytes=ATTN_VMEM),
+        name="attend_backward",
+    )(qkv_b, kv_prompt, kv_prompt, qkv_b, qkv_b, att_b, grad_att, log_totals)
 
 
 def student_loss(stu_rows, pool_query, bias_pool, w_pool, w_class, bias_class, label_value):
@@ -130,8 +324,6 @@
     bias_class,
 ):
     prompt_rows = prompt.shape[1]
-    cont_len = conts.shape[2]
-    prompt_len = prompt_rows * lax.axis_size("shard")
     qkv_low = w_qkv.astype(jnp.bfloat16)
     out_low = w_out.astype(jnp.bfloat16)
     in_low = w_in.astype(jnp.bfloat16)
@@ -147,25 +339,8 @@
     zero_row = jnp.zeros((D,), jnp.float32)
     bias_three = jnp.concatenate([layer_biases[0], zero_row, layer_biases[1]])
     qkv_b = (dot_plain(tokens, qkv_full) + bias_three).astype(jnp.bfloat16)
-    queries = qkv_b[:, :D]
-    keys_own = qkv_b[:, D : 2 * D]
-    values_own = qkv_b[:, 2 * D :]
-    prompt_keys, prompt_values = (
-        lax.all_gather(keys_own[:prompt_rows], "shard", axis=0, tiled=True),
-        lax.all_gather(values_own[:prompt_rows], "shard", axis=0, tiled=True),
-    )
-    keys_all = jnp.concatenate([prompt_keys, keys_own[prompt_rows:]], 0)
-    values_all = jnp.concatenate([prompt_values, values_own[prompt_rows:]], 0)
-    key_pos = jnp.arange(prompt_len + cont_len)
-    query_pos = jnp.concatenate(
-        [
-            lax.axis_index("shard") * prompt_rows + jnp.arange(prompt_rows),
-            prompt_len + jnp.arange(cont_len),
-        ]
-    )
-    allowed = key_pos[None, :] <= query_pos[:, None]
-    attended, log_totals = attend_forward(queries, keys_all, values_all, allowed)
-    att_b = attended.astype(jnp.bfloat16)
+    kv_prompt = lax.all_gather(qkv_b[:prompt_rows, D:], "shard", axis=0, tiled=True)
+    att_b, log_totals = attend_forward(qkv_b, kv_prompt)
     branch = dot_plain(att_b, out_full) + layer_biases[2]
     resid_one = tokens_f + branch
     first = layer_norm(resid_one, norm_gains[0], layer_biases[4])
@@ -227,23 +402,18 @@
     g_outw = dot_first(att_b, g_branch_b)
     g_out_bias = jnp.sum(g_branch_b.astype(jnp.float32), 0)
     g_att_b = dot_second(g_branch_b, out_back).astype(jnp.bfloat16)
-    g_query_rows, g_keys_all, g_values_all = attend_backward(
-        queries, keys_all, values_all, allowed, g_att_b, log_totals
-    )
-    query_grad_b = g_query_rows.astype(jnp.bfloat16)
-    cont_kv_b = jnp.concatenate([g_keys_all[prompt_len:], g_values_all[prompt_len:]], 1).astype(
-        jnp.bfloat16
-    )
-    block_kv_b = jnp.concatenate([g_keys_all[:prompt_len], g_values_all[:prompt_len]], 1).astype(
-        jnp.bfloat16
-    )
+    query_grad_b, g_kp, g_vp, g_kc, g_vc = attend_backward(
+        qkv_b, kv_prompt, att_b, g_att_b, log_totals
+    )
+    cont_kv_b = jnp.concatenate([g_kc, g_vc], 1)
+    block_kv_b = jnp.concatenate([g_kp, g_vp], 1)
     kv_weights = qkv_back[:, D:]
     g_query_w = dot_first(tokens, query_grad_b)
     g_kv_w = dot_first(tokens[prompt_rows:], cont_kv_b)
     g_tokens = g_resid_one + dot_second(query_grad_b, qkv_back[:, :D])
     cont_through = dot_second(cont_kv_b, kv_weights)
     kv_summed = lax.psum_scatter(
-        block_kv_b.astype(jnp.float32).astype(jnp.bfloat16),
+        block_kv_b,
         "shard",
         scatter_dimension=0,
         tiled=True,

time: 1020 us -> 815 us (0.80)
  matrix products: 322 us -> 109 us
  Pallas kernels: 0 us -> 82.1 us
  local copies, waits for them, and re-layouts: 108 us -> 41.9 us
  waiting for transfers between devices: 448 us -> 484 us
  other arithmetic: 50.7 us -> 29.2 us
  loops' own time: 16.2 us -> 0 us
    pallas_call x0 -> x2, Pallas kernels: none -> 82.1 us  [the longest x1 58.9 us: attend_backward(): pl.pallas_call(partial(attend_backward_kernel, prompt_rows, prompt_len),...]
    dot_general x29 -> x5, matrix products: 127 us -> 47.5 us  [dot_plain(): return jnp.dot(left, right, preferred_element_type=jnp.float32)]
    dot_general x42 -> x6, matrix products: 107 us -> 28.4 us  [dot_second(): lax.dot_general(left, right, (((1,), (1,)), ((), ())), preferred_element_...]
    dot_general x30 -> x6, matrix products: 82.1 us -> 27.3 us  [dot_first(): lax.dot_general(left, right, (((0,), (0,)), ((), ())), preferred_element_...]
    all_gather x1, waiting for transfers between devices: 0.02 us -> 30.2 us  [body(): lax.all_gather(in_low, 'shard', axis=0, tiled=True)]
    dynamic_slice x36 -> x0, local copies, waits for them, and re-layouts: 23.1 us -> none  [the longest x24 14 us: attend_forward(): heads, log_totals = lax.map(one_head, jnp.arange(HEADS))]
    dynamic_update_slice x12 -> x0, local copies, waits for them, and re-layouts: 16.4 us -> none  [attend_forward(): heads, log_totals = lax.map(one_head, jnp.arange(HEADS))]
    while x24 -> x0, local copies, waits for them, and re-layouts: 16.3 us -> none
  transfers between devices with their start and end apart: 13 -> 12, of which waited for: 10 -> 11; matrix products, arithmetic and copies ran while one was open for 22% -> 12% of each run, Pallas kernels for 0% -> 3%
where the time goes in v1:
time: 815 us; the launch traced here: 808 us
  waiting for transfers between devices  484 us (59%)
  matrix products  109 us (13%)
  Pallas kernels  82.1 us (10%)
  blocking collectives  43 us (5%)
  local copies, waits for them, and re-layouts  41.9 us (5%)
  other arithmetic  29.2 us (4%)
  between operations  17.9 us (2%)
    psum x1, waiting for transfers between devices, body(): lax.psum((g_biases, g_gains, g_in_bias, g_student, g_vectors, g_pool, g_c...  126 us
    psum x1, waiting for transfers between devices, body(): lax.psum(owned[0].astype(jnp.bfloat16), 'rep').astype(jnp.float32)  87.4 us
    pallas_call x1, Pallas kernels, attend_backward(): pl.pallas_call(partial(attend_backward_kernel, prompt_rows, prompt_len),...  58.9 us
    reduce_scatter x1, waiting for transfers between devices, body(): lax.psum_scatter(g_in.astype(jnp.bfloat16), 'shard', scatter_dimension=0,...  50.5 us
    reduce_scatter x1, waiting for transfers between devices, body(): lax.psum_scatter(g_ffo.astype(jnp.bfloat16), 'shard', scatter_dimension=0...  50.4 us
    dot_general x5, matrix products, dot_plain(): return jnp.dot(left, right, preferred_element_type=jnp.float32)  47.5 us
    psum x1, blocking collectives, body(): lax.psum((g_biases, g_gains, g_in_bias, g_student, g_vectors, g_pool, g_c...  43 us
    unnamed x106, local copies, waits for them, and re-layouts  36.2 us
  transfers between devices with their start and end apart: 12, of which 11 were waited for; matrix products, arithmetic and copies ran while one was open for 12% of the time, Pallas kernels for 3%

profile of v1, /device:TPU:1, one launch (start us, length us, event | category | flops | bytes accessed | tf_op | source)
XLA Modules:
  0.0 807.6 jit_solution(6269098753726537166)
XLA Ops:
  7.3 2.6 convert_element_type.110
  10.5 32.9 %all-gather.6.cloned.1.call-done = bf16[768,2304]{1,0:T(8,128)(2,1)} async-done(((bf16[192,2304]{1,0:T(8,128)(2,1)}), bf16[768,2304]{1,0:T(8,128)(2,1)}) %all-gather.6.cloned.1.call-update) | async-done | bytes 3538960 | tf_op jit(solution)/shard_map/all_gather | solution.py:332
  43.4 5.3 add_convert_fusion.1.q_ref.k_ref.v_ref
  48.7 1.8 copy-done.4
  51.5 1.8 convert_element_type.112
  54.7 2.9 convert_element_type.116
  59.0 21.1 %all-gather.8.cloned.1.call-done.kp_ref.vp_ref = bf16[1024,1536]{1,0:T(8,128)(2,1)} async-done(((bf16[256,1536]{1,0:T(8,128)(2,1)}), bf16[1024,1536]{1,0:T(8,128)(2,1)}) %all-gather.8.cloned.1.call-update) | async-done | bytes 3145744 | tf_op jit(solution)/shard_map/all_gather | solution.py:342
  80.1 23.2 %attend_forward.1 = (bf16[768,768]{1,0:T(8,128)(2,1)S(1)}, f32[768,768]{1,0:T(8,128)S(1)}) custom-call(bf16[768,2304]{1,0:T(8,128)(2,1)} %copy-done.4, bf16[1024,1536]{1,0:T(8,128)(2,1)} %all-gather.8.cloned.1.call-done.kp_ref.vp_ref, bf16[1024,1536]{1,0:T(8,128)(2,1)} %all-gather.8.cloned.1.call-done.kp_ref.vp_ref, bf16[768,2304]{1,0:T(8,128)(2,1)} %copy-done.4, ...), custom_call_target="tpu_custom_call" | custom-call | tf_op jit(solution)/shard_map/attend_forward/pallas_call | solution.py:129
  103.3 1.4 copy-done.2
  104.7 2.6 fusion.57
  107.4 1.4 copy-done.11
  109.0 30.2 %all-gather.12.cloned.1.call-done = bf16[768,3072]{1,0:T(8,128)(2,1)} async-done(((bf16[192,3072]{1,0:T(8,128)(2,1)}), bf16[768,3072]{1,0:T(8,128)(2,1)}) %all-gather.12.cloned.1.call-update) | async-done | bytes 4718608 | tf_op jit(solution)/shard_map/all_gather | solution.py:334
  139.2 30.3 %multiply_convert_fusion = (bf16[768,3072]{1,0:T(8,128)(2,1)}, f32[768,3072]{1,0:T(8,128)}, f32[768,3072]{1,0:T(8,128)}) fusion(f32[3072]{0:T(1024)S(1)} %copy-done.43, bf16[768,3072]{1,0:T(8,128)(2,1)} %all-gather.12.cloned.1.call-done, f32[768,768]{0,1:T(8,128)} %copy-done.11, f32[768]{0:T(1024)S(1)} %get-tuple-element.89, f32[768]{0:T(1024)S(1)} %get-tuple-element.95, ...), kind=kOutput, calls=%fused_computation.4 | convolution fusion | flops 3782541312 | bytes 30695424 | tf_op jit(solution)/shard_map/dot_general | solution.py:23
  169.5 9.1 %all-gather.14.cloned.1.call-done = bf16[3072,768]{1,0:T(8,128)(2,1)} async-done(((bf16[768,768]{1,0:T(8,128)(2,1)}), bf16[3072,768]{1,0:T(8,128)(2,1)}) %all-gather.14.cloned.1.call-update) | async-done | bytes 4718608 | tf_op jit(solution)/shard_map/all_gather | solution.py:335
  178.7 9.0 %fusion.58 = (f32[768]{0:T(1024)S(1)}, f32[768,768]{0,1:T(8,128)S(1)}) fusion(f32[768]{0:T(1024)S(1)} %get-tuple-element.93, bf16[768,3072]{1,0:T(8,128)(2,1)} %get-tuple-element.126, bf16[3072,768]{1,0:T(8,128)(2,1)} %all-gather.14.cloned.1.call-done, f32[768]{0:T(1024)S(1)} %get-tuple-element.89, f32[768]{0:T(1024)S(1)} %get-tuple-element.95, ...), kind=kOutput, calls=%fused_computation.150 | convolution fusion | flops 3628006656 | bytes 14174208 | tf_op jit(solution)/shard_map/dot_general | solution.py:23
  202.0 14.3 %convert_reduce_fusion = (f32[3072]{0:T(1024)S(1)}, bf16[768,3072]{1,0:T(8,128)(2,1)}) fusion(f32[768,3072]{1,0:T(8,128)} %get-tuple-element.127, f32[768,3072]{1,0:T(8,128)} %get-tuple-element.137, f32[3072]{0:T(1024)S(1)} %copy-done.43, bf16[768,768]{0,1:T(8,128)(2,1)S(1)} %get-tuple-element.113, bf16[3072,768]{1,0:T(8,128)(2,1)} %all-gather.14.cloned.1.call-done), kind=kOutput, calls=%fused_computation.2 | convolution fusion | flops 3663983616 | bytes 29515776 | tf_op jit(solution)/shard_map/dot_general | solution.py:33
  216.3 7.0 multiply_reduce_fusion.1
  224.3 1.8 copy-done.42
  227.3 58.9 %attend_backward.1 = (bf16[768,768]{1,0:T(8,128)(2,1)S(1)}, bf16[1024,768]{1,0:T(8,128)(2,1)}, bf16[1024,768]{1,0:T(8,128)(2,1)}, bf16[512,768]{1,0:T(8,128)(2,1)S(1)}, bf16[512,768]{1,0:T(8,128)(2,1)S(1)}) custom-call(bf16[768,2304]{1,0:T(8,128)(2,1)} %copy-done.4, bf16[1024,1536]{1,0:T(8,128)(2,1)} %all-gather.8.cloned.1.call-done.kp_ref.vp_ref, ...), custom_call_target="tpu_custom_call" | custom-call | tf_op jit(solution)/shard_map/attend_backward/pallas_call | solution.py:263
  287.1 3.9 pad_maximum_fusion.1
  291.4 2.2 constant_dynamic-update-slice_fusion.1
  294.5 2.2 convolution_convert_fusion.3
  296.7 31.8 %reduce-scatter.8.cloned.1.call-done = bf16[256,1536]{1,0:T(8,128)(2,1)} async-done(((bf16[1024,1536]{1,0:T(8,128)(2,1)}), bf16[256,1536]{1,0:T(8,128)(2,1)}) %reduce-scatter.8.cloned.1.call-update) | async-done | bytes 786448 | tf_op jit(solution)/shard_map/reduce_scatter | solution.py:415
  328.4 2.1 fusion.21
  330.6 3.0 fusion.6
  333.7 2.0 pad_maximum_fusion
  335.6 5.8 copy.89
  341.5 3.5 convolution_convert_fusion.2
  345.1 9.6 %convolution_convert_fusion.1 = bf16[768,3072]{1,0:T(8,128)(2,1)} fusion(bf16[768,3072]{1,0:T(8,128)(2,1)} %get-tuple-element.111, f32[768,768]{0,1:T(8,128)} %copy-done.11, f32[768]{0:T(1024)S(1)} %get-tuple-element.89, f32[768]{0:T(1024)S(1)} %get-tuple-element.95, f32[768]{0:T(1024)S(1)} %fusion.35, f32[768]{0:T(1024)S(1)} %broadcast_multiply_fusion.3), kind=kOutput, calls=%fused_computation.20 | convolution fusion | flops 3629187072 | bytes 11808768 | tf_op jit(solution)/shard_map/dot_general | solution.py:27
  355.9 8.0 convolution_convert_fusion
  363.9 18.1 %reduce-scatter.16.cloned.1.call-done = bf16[192,2304]{1,0:T(8,128)(2,1)} async-done(((bf16[768,2304]{1,0:T(8,128)(2,1)}), bf16[192,2304]{1,0:T(8,128)(2,1)}) %reduce-scatter.16.cloned.1.call-update) | async-done | bytes 884752
  382.0 2.3 copy.90
  384.3 25.9 %reduce-scatter.10.cloned.1.call-done = bf16[192,768]{1,0:T(8,128)(2,1)} async-done(((bf16[768,768]{1,0:T(8,128)(2,1)}), bf16[192,768]{1,0:T(8,128)(2,1)}) %reduce-scatter.10.cloned.1.call-update) | async-done | bytes 294928 | tf_op jit(solution)/shard_map/reduce_scatter | solution.py:443
  410.2 50.5 %reduce-scatter.12.cloned.1.call-done = bf16[192,3072]{1,0:T(8,128)(2,1)} async-done(((bf16[768,3072]{1,0:T(8,128)(2,1)}), bf16[192,3072]{1,0:T(8,128)(2,1)}) %reduce-scatter.12.cloned.1.call-update) | async-done | bytes 1179664 | tf_op jit(solution)/shard_map/reduce_scatter | solution.py:446
  460.7 50.4 %reduce-scatter.14.cloned.1.call-done = bf16[768,768]{1,0:T(8,128)(2,1)} async-done(((bf16[3072,768]{1,0:T(8,128)(2,1)}), bf16[768,768]{1,0:T(8,128)(2,1)}) %reduce-scatter.14.cloned.1.call-update) | async-done | bytes 1179664 | tf_op jit(solution)/shard_map/reduce_scatter | solution.py:449
  513.3 2.3 copy.72
  516.4 1.9 copy.71
  520.5 4.5 fusion.7
  527.9 1.4 copy-done.13
  529.5 1.6 copy.74
  533.5 43.0 %all-reduce.1 = (f32[6,768]{1,0:T(8,128)}, f32[2,768]{1,0:T(2,128)}, f32[3072]{0:T(1024)}, f32[3,128]{1,0:T(4,128)}, f32[128,14]{0,1:T(8,128)}, /*index=5*/f32[14]{0:T(128)}) all-reduce(f32[6,768]{1,0:T(8,128)S(1)} %stack.32, f32[2,768]{1,0:T(2,128)S(1)} %pad_maximum_fusion.6, ...), channel_id=1, replica_groups=mesh['rep'=8,'shard'=4] {'rep','shard'}, use_global_device_ids=true, to_apply=%region_33.34 | all-reduce | flops 11406 | bytes 91248 | tf_op jit(solution)/shard_map/psum | solution.py:464
  576.5 87.4 %all-reduce.9.cloned.1.call-done = (bf16[192,2304]{0,1:T(8,128)(2,1)}, bf16[192,768]{1,0:T(8,128)(2,1)}, bf16[192,3072]{1,0:T(8,128)(2,1)}, bf16[768,768]{1,0:T(8,128)(2,1)}) async-done(((bf16[192,2304]{0,1:T(8,128)(2,1)}, bf16[192,768]{1,0:T(8,128)(2,1)}, bf16[192,3072]{1,0:T(8,128)(2,1)}, bf16[768,768]{1,0:T(8,128)(2,1)}), (bf16[192,2304]{0,1:T(8,128)(2,1)}, bf16[192,768]{1,0:T(8,128)(2,1)}, ...) | async-done | bytes 3538960 | tf_op jit(solution)/shard_map/psum | solution.py:454
  663.9 3.0 convert_element_type.132
  666.9 1.6 convert_element_type.134
  668.6 1.5 copy.75
  671.0 126.4 %all-reduce.7.cloned.1.call-done = (f32[768,128]{1,0:T(8,128)}, f32[128,128]{1,0:T(8,128)}) async-done(((f32[768,128]{1,0:T(8,128)}, f32[128,128]{1,0:T(8,128)}), (f32[768,128]{1,0:T(8,128)}, f32[128,128]{1,0:T(8,128)})) %all-reduce.7.cloned.1.call-update) | async-done | bytes 458768 | tf_op jit(solution)/shard_map/psum | solution.py:464
  797.4 1.8 copy.115
  799.1 1.5 copy.116
  (200 shorter events, 33.3 us)
Async XLA Ops:
  7.2 184.3 %copy-start = (f32[128,128]{1,0:T(8,128)S(1)}, f32[128,128]{1,0:T(8,128)}, u32[]{:S(2)}) copy-start(f32[128,128]{1,0:T(8,128)} %param.31) | copy-start | bytes 196612
  7.2 2.7 copy-start.15
  7.2 3.0 copy-start.18
  7.2 3.2 copy-start.37
  7.2 36.2 %all-gather.6.cloned.1.call-start = ((), (), s32[]{:S(2)}) async-start(), calls=%async_computation.5 | async-start | bytes 4423680 | tf_op jit(solution)/shard_map/all_gather | solution.py:332
  9.9 70.3 %all-gather.8.cloned.1.call-start = ((), (), s32[]{:S(2)}) async-start(), calls=%async_computation.6 | async-start | bytes 3932160 | tf_op jit(solution)/shard_map/all_gather | solution.py:342
  10.2 94.5 %copy-start.29 = (bf16[1,1,512,768]{2,3,1,0:T(8,128)(2,1)}, bf16[1,1,512,768]{2,3,1,0:T(8,128)(2,1)S(1)}, u32[]{:S(2)}) copy-start(bf16[1,1,512,768]{2,3,1,0:T(8,128)(2,1)S(1)} %copy.63) | copy-start | bytes 2359300
  10.4 33.0 %copy-start.32 = (bf16[1,256,768]{1,2,0:T(8,128)(2,1)}, bf16[1,256,768]{1,2,0:T(8,128)(2,1)S(1)}, u32[]{:S(2)}) copy-start(bf16[1,256,768]{1,2,0:T(8,128)(2,1)S(1)} %copy.62) | copy-start | bytes 1179652
  48.7 1.8 copy-start.4
  50.5 2.9 copy-start.17
  51.5 53.3 %all-gather.10.cloned.1.call-start = ((), (), s32[]{:S(2)}) async-start(), calls=%async_computation.7 | async-start | bytes 1474560 | tf_op jit(solution)/shard_map/all_gather | solution.py:333
  53.4 85.8 %all-gather.12.cloned.1.call-start = ((), (), s32[]{:S(2)}) async-start(), calls=%async_computation.8 | async-start | bytes 5898240 | tf_op jit(solution)/shard_map/all_gather | solution.py:334
  54.6 3.1 copy-start.38
  54.6 3.1 copy-start.39
  54.6 3.9 copy-start.28
  54.6 4.2 copy-start.31
  54.7 124.0 %all-gather.14.cloned.1.call-start = ((), (), s32[]{:S(2)}) async-start(), calls=%async_computation.9 | async-start | bytes 5898240 | tf_op jit(solution)/shard_map/all_gather | solution.py:335
  57.6 270.8 %reduce-scatter.8.cloned.1.call-start = ((), (), s32[]{:S(2)}) async-start(), calls=%async_computation.10 | async-start | bytes 3932160 | tf_op jit(solution)/shard_map/reduce_scatter | solution.py:415
  107.4 31.9 %copy-start.43 = (f32[3072]{0:T(1024)S(1)}, f32[3072]{0:T(1024)}, u32[]{:S(2)}) copy-start(f32[3072]{0:T(1024)} %param.28) | copy-start | bytes 36868
  188.0 2.1 copy-start.19
  188.0 3.7 copy-start.36
  188.0 3.7 copy-start.41
  192.5 8.5 %copy-start.40 = (f32[14]{0:T(128)}, f32[14]{0:T(128)S(1)}, u32[]{:S(2)}) copy-start(f32[14]{0:T(128)S(1)} %get-tuple-element.141) | copy-start | bytes 172
  198.1 1.7 copy-start.6
  199.1 1.8 copy-start.25
  201.7 14.6 %slice-start = ((s8[4718592]{0:T(1024)(128)(4,1)}), s8[4194304]{0:T(1024)(128)(4,1)S(1)}, s32[]{:S(2)}) async-start(s8[4718592]{0:T(1024)(128)(4,1)} %bitcast.161), calls=%async_computation.17 | async-start | bytes 8388608
  202.0 14.3 %copy-start.21 = (bf16[768,768]{0,1:T(8,128)(2,1)}, bf16[768,768]{0,1:T(8,128)(2,1)S(1)}, u32[]{:S(2)}) copy-start(bf16[768,768]{0,1:T(8,128)(2,1)S(1)} %get-tuple-element.113) | copy-start | bytes 3538948
  202.0 14.3 %copy-start.12 = (f32[768,768]{0,1:T(8,128)S(1)}, f32[768,768]{0,1:T(8,128)}, u32[]{:S(2)}) copy-start(f32[768,768]{0,1:T(8,128)} %copy-done.11) | copy-start | bytes 7077892
  202.0 14.3 %slice-start.1 = ((s8[4718592]{0:T(1024)(128)(4,1)}), s8[524288]{0:T(1024)(128)(4,1)S(1)}, s32[]{:S(2)}) async-start(s8[4718592]{0:T(1024)(128)(4,1)} %bitcast.161), calls=%async_computation.18 | async-start | bytes 1048576
  224.0 3.3 copy-start.7
  224.0 2.1 copy-start.42
  224.3 3.0 copy-start.23
  291.0 91.0 %reduce-scatter.16.cloned.1.call-start = ((), (), s32[]{:S(2)}) async-start(), calls=%async_computation.14 | async-start | bytes 4423680
  291.4 3.1 copy-start.30
  291.4 3.1 copy-start.33
  328.4 2.1 copy-start.16
  330.6 3.1 copy-start.24
  341.5 68.7 %reduce-scatter.10.cloned.1.call-start = ((), (), s32[]{:S(2)}) async-start(), calls=%async_computation.11 | async-start | bytes 1474560 | tf_op jit(solution)/shard_map/reduce_scatter | solution.py:443
  345.0 115.7 %reduce-scatter.12.cloned.1.call-start = ((), (), s32[]{:S(2)}) async-start(), calls=%async_computation.12 | async-start | bytes 5898240 | tf_op jit(solution)/shard_map/reduce_scatter | solution.py:446
  354.6 156.5 %reduce-scatter.14.cloned.1.call-start = ((), (), s32[]{:S(2)}) async-start(), calls=%async_computation.13 | async-start | bytes 5898240 | tf_op jit(solution)/shard_map/reduce_scatter | solution.py:449
  363.9 300.0 %all-reduce.9.cloned.1.call-start = ((), (), s32[]{:S(2)}) async-start(), calls=%async_computation.16 | async-start | bytes 7667712 | tf_op jit(solution)/shard_map/psum | solution.py:454
  511.1 286.2 %all-reduce.7.cloned.1.call-start = ((), (), s32[]{:S(2)}) async-start(), calls=%async_computation.15 | async-start | bytes 917504 | tf_op jit(solution)/shard_map/psum | solution.py:464
  513.3 6.0 copy-start.26
  520.4 4.6 copy-start.14
  520.5 4.7 copy-start.34
  663.9 3.0 copy-start.20
  666.9 1.7 copy-start.27
  668.5 132.1 %copy-start.1 = (f32[128,128]{1,0:T(8,128)S(1)}, f32[128,128]{1,0:T(8,128)}, u32[]{:S(2)}) copy-start(f32[128,128]{1,0:T(8,128)} %param.31) | copy-start | bytes 196612
  (10 other events, 13.3 us)
Sparse Core Ops, SparseCore 0:
  10.2 33.1 all-gather.5
  51.6 28.4 all-gather.7
  82.3 17.4 all-gather.9
  101.7 37.4 all-gather.11
  141.2 37.4 all-gather.13
  291.1 37.3 reduce-scatter.7
  341.6 40.3 reduce-scatter.15
  384.6 25.6 reduce-scatter.9
  412.7 47.9 reduce-scatter.11
  463.1 47.9 reduce-scatter.13
  515.7 148.1 all-reduce.8
  669.7 127.6 all-reduce.6
